TPU v7x, 128 devices: a whole 4x4x4 slice. The times are simulated.
128 devices in a mesh: fld: 1, col: 2 (over core), row: 64 (over z, y, x).
Axes of the slice: x: 4, y: 4, z: 4, core: 2. Of those that a mesh axis runs over, the one named last changes fastest.
Arguments:
- u_real: float32 [4, 256, 256, 256], P('fld', None, 'row', 'col')
- u_imag: float32 [4, 256, 256, 256], P('fld', None, 'row', 'col')
- g_filter: float32 [256, 256, 256], P('row', 'col')
Outputs:
- output 1: float32 [4, 256, 256, 256], P('fld', 'row', 'col')
- output 2: float32 [4, 256, 256, 256], P('fld', 'row', 'col')
All inputs are finite; a program needn't handle non-finite values.
Results may differ from a plain program's by a relative error of at most 0.001.
Values are sent between devices in bfloat16 or wider.
A program may use at most 1 GiB of HBM per device.

v0:
```python
import math
import jax
import jax.numpy as jnp
from jax import lax
from jax.sharding import PartitionSpec as P, NamedSharding


def dft_block(length):
    positions = jnp.arange(length)
    phase_steps = (positions[:, None] * positions[None, :]) % length
    angles = phase_steps.astype(jnp.float32) * (2.0 * math.pi / length)
    norm_scale = 1.0 / math.sqrt(length)
    cos_part = jnp.cos(angles) * norm_scale
    sin_part = jnp.sin(angles) * norm_scale
    real_rows = jnp.stack([cos_part, sin_part], axis=1)
    imag_rows = jnp.stack([-sin_part, cos_part], axis=1)
    return jnp.stack([real_rows, imag_rows])


def solution(mesh):
    highest = lax.Precision.HIGHEST

    def local_forward(u_real, u_imag, g_filter):
        dft_mat = dft_block(u_real.shape[1])
        field_pair = jnp.stack([u_real, u_imag])
        field_pair = jnp.einsum("dkcx,cbxyz->dbkyz", dft_mat, field_pair, precision=highest, preferred_element_type=jnp.float32)
        field_pair = lax.all_to_all(field_pair, "row", 2, 3, tiled=True)
        field_pair = jnp.einsum("dkcy,cbxyz->dbxkz", dft_mat, field_pair, precision=highest, preferred_element_type=jnp.float32)
        field_pair = lax.all_to_all(field_pair, "col", 3, 4, tiled=True)
        field_pair = jnp.einsum("dkcz,cbxyz->dbxyk", dft_mat, field_pair, precision=highest, preferred_element_type=jnp.float32)
        filtered = field_pair * g_filter
        return filtered[0], filtered[1]

    field_spec = P("fld", None, "row", "col")
    out_spec = P("fld", "row", "col", None)
    return jax.shard_map(local_forward, mesh=mesh, in_specs=(field_spec, field_spec, P("row", "col", None)), out_specs=(out_spec, out_spec), check_vma=False)
```

profile of v0, /device:TPU:3, one launch (start us, length us, event | category | flops | bytes accessed | tf_op | source)
XLA Modules:
  0.0 158.7 jit_solution(18287977174777346632)
XLA Ops:
  0.6 1.0 fusion.20
  1.6 1.8 %sine_multiply_fusion = (f32[256,1,256]{2,0,1:T(8,128)}, f32[256,1,256]{2,0,1:T(8,128)}) fusion(), kind=kLoop, calls=%fused_computation.24 | loop fusion | flops 1048576 | bytes 524288 | tf_op jit(solution)/shard_map/mul | solution.py:14
  3.4 1.9 %copy.15 = f32[4,256,4,128]{1,3,2,0:T(8,128)S(1)} copy(f32[4,256,4,128]{3,2,1,0:T(4,128)} %param.3) | data formatting | bytes 4194304 | tf_op args[0]
  5.3 2.9 %copy.16 = f32[4,256,4,128]{1,3,2,0:T(8,128)} copy(f32[4,256,4,128]{3,2,1,0:T(4,128)} %param.4) | data formatting | bytes 4194304 | tf_op args[1]
  8.2 1.2 maximum_bitcast_fusion.8
  9.4 9.6 %fusion.8 = f32[2,4,256,4,128]{2,4,0,3,1:T(8,128)} fusion(f32[1,4,256,4,128]{2,4,0,3,1:T(8,128)} %bitcast.63, f32[1,4,256,4,128]{2,4,0,3,1:T(8,128)S(1)} %bitcast.62, f32[1,256,2,256]{3,1,2,0:T(8,128)S(1)} %get-tuple-element.5, f32[1,256,2,256]{3,1,2,0:T(8,128)S(1)} %get-tuple-element.4), kind=kOutput, calls=%fused_computation.11 | convolution fusion | flops 6443761664 | bytes 9437184 | tf_op jit(solution)/shard_map/dkcx,cbxyz->dbkyz/dot_general | solution.py:26
  19.0 7.3 %copy.17 = f32[2,4,256,4,128]{4,0,3,1,2:T(2,128)} copy(f32[2,4,256,4,128]{2,4,0,3,1:T(8,128)} %fusion.8) | data formatting | bytes 8388608 | tf_op jit(solution)/shard_map/dkcx,cbxyz->dbkyz/transpose | solution.py:26
  26.3 73.3 %all_to_all.36 = f32[2,4,256,4,128]{4,0,3,1,2:T(2,128)S(1)} all-to-all(f32[2,4,256,4,128]{4,0,3,1,2:T(2,128)} %copy.17), channel_id=1, replica_groups=mesh['fld'=1,'col'=2,'row'=64] {'row'}, dimensions={2} | all-to-all | bytes 8388608 | tf_op jit(solution)/shard_map/all_to_all | solution.py:27
  99.6 2.4 %copy.18 = f32[2,4,256,4,128]{4,2,3,1,0:T(8,128)S(1)} copy(f32[2,4,256,4,128]{4,0,3,1,2:T(2,128)S(1)} %all_to_all.36) | data formatting | bytes 8388608 | tf_op jit(solution)/shard_map/all_to_all | solution.py:27
  102.0 3.0 %copy.19 = f32[2,4,4,64,4,128]{5,4,3,2,1,0:T(4,128)S(1)} copy(f32[2,4,4,64,4,128]{5,2,3,4,1,0:T(4,128)S(1)} %bitcast.58) | data formatting | bytes 8388608 | tf_op jit(solution)/shard_map/all_to_all | solution.py:27
  105.0 15.3 %fusion.9 = f32[2,4,4,256,128]{3,4,0,2,1:T(8,128)} fusion(f32[2,4,4,256,128,1]{4,3,2,1,0,5:T(8,128)S(1)} %bitcast.59, f32[1,256,2,256]{3,1,2,0:T(8,128)S(1)} %get-tuple-element.5, f32[1,256,2,256]{3,1,2,0:T(8,128)S(1)} %get-tuple-element.4), kind=kOutput, calls=%fused_computation.12 | convolution fusion | flops 6442713088 | bytes 9437184 | tf_op jit(solution)/shard_map/dkcy,cbxyz->dbxkz/dot_general | solution.py:28
  120.3 7.3 %copy.21 = f32[2,4,4,256,128]{4,0,2,1,3:T(2,128)} copy(f32[2,4,4,256,128]{3,4,0,2,1:T(8,128)} %fusion.9) | data formatting | bytes 8388608 | tf_op jit(solution)/shard_map/dkcy,cbxyz->dbxkz/transpose | solution.py:28
  127.6 8.5 %all_to_all.37 = f32[2,4,4,256,128]{4,0,2,1,3:T(2,128)S(1)} all-to-all(f32[2,4,4,256,128]{4,0,2,1,3:T(2,128)} %copy.21), channel_id=1, replica_groups=mesh['fld'=1,'col'=2,'row'=64] {'col'}, dimensions={3} | all-to-all | bytes 8388608 | tf_op jit(solution)/shard_map/all_to_all | solution.py:29
  136.1 5.2 %copy.37 = f32[2,4,4,2,128,128]{5,3,4,0,2,1:T(2,128)} copy(f32[2,4,4,2,128,128]{5,0,2,1,4,3:T(2,128)S(1)} %bitcast.60) | data formatting | bytes 8388608 | tf_op jit(solution)/shard_map/all_to_all | solution.py:29
  141.3 0.0 copy-start
  141.3 6.5 %reshape.91 = f32[2,4,4,128,256,1]{4,3,0,2,1,5:T(8,128)} reshape(f32[2,4,4,128,2,128]{5,4,3,0,2,1:T(2,128)} %bitcast.61) | data formatting | bytes 8388608 | tf_op jit(solution)/shard_map/all_to_all | solution.py:29
  147.8 0.0 copy-done
  147.8 8.6 %fusion.3 = f32[2,4,4,128,256]{4,3,0,2,1:T(8,128)S(1)} fusion(f32[2,4,4,128,256,1]{4,3,0,2,1,5:T(8,128)} %reshape.91, f32[4,128,256]{2,1,0:T(8,128)S(1)} %copy-done, f32[1,256,2,256]{3,1,2,0:T(8,128)S(1)} %get-tuple-element.5, f32[1,256,2,256]{3,1,2,0:T(8,128)S(1)} %get-tuple-element.4), kind=kOutput, calls=%fused_computation.5 | convolution fusion | flops 6443761664 | bytes 9961472 | tf_op jit(solution)/shard_map/dkcz,cbxyz->dbxyk/dot_general | solution.py:30
  156.3 2.4 %slice_bitcast_fusion = (f32[4,4,128,256]{3,2,1,0:T(8,128)}, f32[4,4,128,256]{3,2,1,0:T(8,128)}) fusion(f32[2,4,4,128,256]{4,3,0,2,1:T(8,128)S(1)} %fusion.3), kind=kLoop, calls=%fused_computation.13 | loop fusion | bytes 8388608 | tf_op jit(solution)/shard_map/squeeze | solution.py:32
Async XLA Ops:
  141.3 6.5 %copy-start = (f32[4,128,256]{2,1,0:T(8,128)S(1)}, f32[4,128,256]{2,1,0:T(8,128)}, u32[]{:S(2)}) copy-start(f32[4,128,256]{2,1,0:T(8,128)} %param.5) | copy-start | bytes 1572868
where the time goes:
time: 159 us
  blocking collectives  81.8 us (51%)
  local copies, waits for them, and re-layouts  38.8 us (24%)
  matrix products  33.5 us (21%)
  other arithmetic  3.94 us (2%)
    all_to_all x1, blocking collectives, local_forward(): field_pair = lax.all_to_all(field_pair, 'row', 2, 3, tiled=True)  73.3 us
    dot_general x1, matrix products, local_forward(): jnp.einsum('dkcy,cbxyz->dbxkz', dft_mat, field_pair, precision=highest, p...  15.3 us
    all_to_all x2, local copies, waits for them, and re-layouts, local_forward(): field_pair = lax.all_to_all(field_pair, 'col', 3, 4, tiled=True)  11.7 us
    dot_general x1, matrix products, local_forward(): jnp.einsum('dkcx,cbxyz->dbkyz', dft_mat, field_pair, precision=highest, p...  9.59 us
    dot_general x1, matrix products, local_forward(): jnp.einsum('dkcz,cbxyz->dbxyk', dft_mat, field_pair, precision=highest, p...  8.57 us
    all_to_all x1, blocking collectives, local_forward(): field_pair = lax.all_to_all(field_pair, 'col', 3, 4, tiled=True)  8.46 us
    transpose x1, local copies, waits for them, and re-layouts, local_forward(): jnp.einsum('dkcy,cbxyz->dbxkz', dft_mat, field_pair, precision=highest, p...  7.3 us
    transpose x1, local copies, waits for them, and re-layouts, local_forward(): jnp.einsum('dkcx,cbxyz->dbkyz', dft_mat, field_pair, precision=highest, p...  7.3 us

commit v1 on v0

v1 whole, which is shorter than its diff:
```python
import random

import jax
import jax.numpy as jnp
import numpy as np
from jax import lax
from jax.experimental import pallas as pl
from jax.experimental.pallas import tpu as pltpu
from jax.sharding import PartitionSpec as P

MESH = pl.DeviceIdType.MESH
N = 256
FIELDS = 4
HIGHEST = lax.Precision.HIGHEST
F32 = jnp.float32


def dft_blocks():
    steps = np.outer(np.arange(N), np.arange(N)) % N
    angles = steps * (2.0 * np.pi / N)
    cos_part, sin_part = np.cos(angles) / np.sqrt(N), np.sin(angles) / np.sqrt(N)
    real_rows = np.stack([cos_part, sin_part], axis=1)
    imag_rows = np.stack([-sin_part, cos_part], axis=1)
    return np.stack([real_rows, imag_rows])


def matrices():
    full = dft_blocks()
    x_mat = full.reshape(2, 64, 4, 2, N).transpose(1, 0, 2, 3, 4).reshape(512, 512)
    y_mat = full.reshape(2, 2, 128, 2, 64, 4).transpose(1, 0, 2, 3, 5, 4).reshape(512, 512)
    z_mat = full.transpose(2, 3, 0, 1).reshape(512, 512)
    return [m.astype(np.float32) for m in (x_mat, y_mat, z_mat)]


def link_use(offset):
    use = [0] * 6
    for k in range(3):
        if offset[k] in (1, 2):
            use[2 * k] += 1
        if offset[k] in (3, 2):
            use[2 * k + 1] += 1
    return use


def send_order(seed=0):
    rng = random.Random(seed)
    left = [(s % 4, (s // 4) % 4, s // 16) for s in range(1, 64)]
    rng.shuffle(left)
    total, order = [0] * 6, []
    while left:

        def cost(offset):
            after = [a + b for a, b in zip(total, link_use(offset))]
            mean = sum(after) / 6
            return max(after) - min(after), sum((v - mean) ** 2 for v in after), -sum(link_use(offset))

        best = min(left, key=cost)
        left.remove(best)
        order.append(best)
        total = [a + b for a, b in zip(total, link_use(best))]
    return order


ORDER = send_order()


def kernel(ur_hbm, ui_hbm, g_hbm, xm_hbm, ym_hbm, zm_hbm, wr_hbm, wi_hbm,
           u_buf, xm, ym, zm, g_buf, cols, send, recv, planes, ysend, zbuf, wbuf,
           in_sem, send_sem, recv_sem, pair_send, pair_recv, out_sem):
    row, col = lax.axis_index("row"), lax.axis_index("col")
    cz, cy, cx = row // 16, (row // 4) % 4, row % 4
    sign = 1 - 2 * col

    def peer(offset):
        dx, dy, dz = offset
        return ((cz + sign * dz + 4) % 4) * 16 + ((cy + sign * dy + 4) % 4) * 4 + (cx + sign * dx + 4) % 4

    barrier = pltpu.get_barrier_semaphore()
    for offset in ORDER:
        pl.semaphore_signal(barrier, 1, device_id=(0, col, peer(offset)), device_id_type=MESH)
    pl.semaphore_signal(barrier, 1, device_id=(0, 1 - col, row), device_id_type=MESH)

    def load_u(f, part):
        src = (ur_hbm, ui_hbm)[part]
        return pltpu.make_async_copy(src.at[f], u_buf.at[f, part], in_sem.at[2 * f + part])

    x_load = pltpu.make_async_copy(xm_hbm, xm, in_sem.at[8])
    y_load = pltpu.make_async_copy(ym_hbm, ym, in_sem.at[9])
    z_load = pltpu.make_async_copy(zm_hbm, zm, in_sem.at[10])
    g_load = pltpu.make_async_copy(g_hbm, g_buf, in_sem.at[11])
    load_u(0, 0).start()
    load_u(0, 1).start()
    x_load.start()
    for f in range(1, FIELDS):
        load_u(f, 0).start()
        load_u(f, 1).start()
    y_load.start()
    z_load.start()
    g_load.start()
    x_load.wait()

    def x_step(f):
        load_u(f, 0).wait()
        load_u(f, 1).wait()
        for half in range(2):
            for part in range(2):
                for k in range(2):
                    cols[pl.ds(part * 256, 256), pl.ds(k * 128, 128)] = u_buf[f, part, pl.ds(2 * half + k, 256, stride=4), :]
            out = jnp.dot(xm[...], cols[...], precision=HIGHEST, preferred_element_type=F32)
            send[f, 2 * half] = out[:, :128]
            send[f, 2 * half + 1] = out[:, 128:]

    mine = pl.ds(pl.multiple_of(row * 8, 8), 8)

    def send_field(f):
        for offset in ORDER:
            to = peer(offset)
            pltpu.make_async_remote_copy(
                src_ref=send.at[f, :, pl.ds(pl.multiple_of(to * 8, 8), 8), :],
                dst_ref=recv.at[f, :, mine, :],
                send_sem=send_sem.at[f],
                recv_sem=recv_sem.at[f],
                device_id=(0, col, to),
                device_id_type=MESH,
            ).start()
        for yy in range(4):
            recv[f, yy, mine, :] = send[f, yy, mine, :]

    x_step(0)
    pl.semaphore_wait(barrier, len(ORDER) + 1)
    send_field(0)

    @pl.loop(1, FIELDS)
    def _(f):
        x_step(f)
        send_field(f)

    y_load.wait()
    z_load.wait()
    g_load.wait()
    other = 1 - col

    def pair_copy(f, p):
        return pltpu.make_async_remote_copy(
            src_ref=ysend.at[f, p],
            dst_ref=zbuf.at[f, p, col],
            send_sem=pair_send.at[2 * f + p],
            recv_sem=pair_recv.at[2 * f + p],
            device_id=(0, other, row),
            device_id_type=MESH,
        )

    def y_step(f, p):
        for part in range(2):
            for yy in range(4):
                for k in range(2):
                    planes[pl.ds(part * 256 + yy * 64, 64), pl.ds(k * 128, 128)] = recv[f, yy, pl.ds(part * 4 + 2 * p + k, 64, stride=8), :]
        theirs = jnp.dot(ym[pl.ds(pl.multiple_of(other * 256, 256), 256), :], planes[...], precision=HIGHEST, preferred_element_type=F32)
        for part in range(2):
            for k in range(2):
                ysend[f, p, part, pl.ds(k * 128, 128), :] = theirs[part * 128 : part * 128 + 128, k * 128 : k * 128 + 128]
        pair_copy(f, p).start()
        ours = jnp.dot(ym[pl.ds(pl.multiple_of(col * 256, 256), 256), :], planes[...], precision=HIGHEST, preferred_element_type=F32)
        for part in range(2):
            for k in range(2):
                zbuf[f, p, col, part, pl.ds(k * 128, 128), :] = ours[part * 128 : part * 128 + 128, k * 128 : k * 128 + 128]

    def out_copies(f, p):
        return [
            pltpu.make_async_copy(wbuf.at[f, part, pl.ds(2 * p, 2)], (wr_hbm, wi_hbm)[part].at[f, pl.ds(2 * p, 2)], out_sem.at[2 * f + p, part])
            for part in range(2)
        ]

    def z_step(f, p):
        pair_copy(f, p).wait_recv()
        lines = jnp.concatenate([zbuf[f, p, h, part] for part in range(2) for h in range(2)], axis=1)
        out = jnp.dot(lines, zm[...], precision=HIGHEST, preferred_element_type=F32)
        for part in range(2):
            for k in range(2):
                wbuf[f, part, 2 * p + k] = out[k * 128 : k * 128 + 128, part * 256 : part * 256 + 256] * g_buf[2 * p + k]
        for copy in out_copies(f, p):
            copy.start()

    @pl.loop(0, FIELDS)
    def _(f):
        pltpu.make_async_copy(recv.at[f, :, pl.ds(0, 504), :], recv.at[f, :, pl.ds(0, 504), :], recv_sem.at[f]).wait()
        y_step(f, 0)

        @pl.when(f > 0)
        def _():
            z_step(f - 1, 1)

        y_step(f, 1)
        z_step(f, 0)

    z_step(FIELDS - 1, 1)

    @pl.loop(0, FIELDS)
    def _(f):
        pltpu.make_async_copy(send.at[f, :, pl.ds(0, 504), :], send.at[f, :, pl.ds(0, 504), :], send_sem.at[f]).wait()
        for p in range(2):
            pair_copy(f, p).wait_send()
            for copy in out_copies(f, p):
                copy.wait()


def solution(mesh):
    mats = matrices()

    def local_forward(u_real, u_imag, g_filter):
        flat = (FIELDS, 4 * N, 128)
        any_spec = pl.BlockSpec(memory_space=pl.ANY)
        hbm_spec = pl.BlockSpec(memory_space=pltpu.HBM)
        out = jax.ShapeDtypeStruct((FIELDS, 4, 128, N), F32)
        return pl.pallas_call(
            kernel,
            out_shape=(out, out),
            in_specs=[hbm_spec] * 6,
            out_specs=(hbm_spec, hbm_spec),
            scratch_shapes=[
                pltpu.VMEM((FIELDS, 2, 4 * N, 128), F32),
                pltpu.VMEM((512, 512), F32),
                pltpu.VMEM((512, 512), F32),
                pltpu.VMEM((512, 512), F32),
                pltpu.VMEM((4, 128, N), F32),
                pltpu.VMEM((512, 256), F32),
                pltpu.VMEM((FIELDS, 4, 512, 128), F32),
                pltpu.VMEM((FIELDS, 4, 512, 128), F32),
                pltpu.VMEM((512, 256), F32),
                pltpu.VMEM((FIELDS, 2, 2, 256, 128), F32),
                pltpu.VMEM((FIELDS, 2, 2, 2, 256, 128), F32),
                pltpu.VMEM((FIELDS, 2, 4, 128, N), F32),
                pltpu.SemaphoreType.DMA((12,)),
                pltpu.SemaphoreType.DMA((FIELDS,)),
                pltpu.SemaphoreType.DMA((FIELDS,)),
                pltpu.SemaphoreType.DMA((2 * FIELDS,)),
                pltpu.SemaphoreType.DMA((2 * FIELDS,)),
                pltpu.SemaphoreType.DMA((2 * FIELDS, 2)),
            ],
            compiler_params=pltpu.CompilerParams(collective_id=0, has_side_effects=True, vmem_limit_bytes=56 * 2**20),
        )(u_real.reshape(flat), u_imag.reshape(flat), g_filter, *[jnp.asarray(m) for m in mats])

    field_spec = P("fld", None, "row", "col")
    out_spec = P("fld", "row", "col", None)
    return jax.shard_map(local_forward, mesh=mesh, in_specs=(field_spec, field_spec, P("row", "col", None)), out_specs=(out_spec, out_spec), check_vma=False)
```

time: 159 us -> 84.7 us (0.53)
  the two profiles are of different devices: /device:TPU:3 before, /device:TPU:1 now
where the time goes in v1:
time: 84.7 us; the launch traced here: 84.6 us
  Pallas kernels  79.4 us (94%)
  local copies, waits for them, and re-layouts  4.57 us (5%)
    pallas_call x1, Pallas kernels, local_forward(): pl.pallas_call(kernel, out_shape=(out, out), in_specs=[hbm_spec] * 6, out...  79.4 us
    unnamed x4, local copies, waits for them, and re-layouts  4.57 us

profile of v1, /device:TPU:1, one launch (start us, length us, event | category | flops | bytes accessed | tf_op | source)
XLA Modules:
  0.0 84.6 jit_solution(8455588209873956349)
XLA Ops:
  0.6 79.4 %shard_map.77 = (f32[4,4,128,256]{3,2,1,0:T(8,128)}, f32[4,4,128,256]{3,2,1,0:T(8,128)}) custom-call(f32[4,1024,128]{2,1,0:T(8,128)} %bitcast.2, f32[4,1024,128]{2,1,0:T(8,128)} %bitcast.3, f32[4,128,256]{2,1,0:T(8,128)} %g_hbm.1, f32[512,512]{1,0:T(8,128)} %constant.6.clone.xm_hbm, f32[512,512]{1,0:T(8,128)} %constant.7.clone.ym_hbm, ...), custom_call_target="tpu_custom_call" | custom-call | tf_op jit(solution)/shard_map/pallas_call | solution.py:215
  80.0 0.0 copy-start
  80.0 3.2 %copy.10 = f32[4,4,128,256]{3,2,1,0:T(8,128)} copy(f32[4,4,128,256]{3,2,1,0:T(8,128)} %get-tuple-element.4) | data formatting | bytes 4194304
  83.2 0.0 copy-done
  83.2 1.3 %copy.11 = f32[4,4,128,256]{3,2,1,0:T(8,128)} copy(f32[4,4,128,256]{3,2,1,0:T(8,128)S(1)} %copy-done) | data formatting | bytes 4194304
Async XLA Ops:
  80.0 3.3 %copy-start = (f32[4,4,128,256]{3,2,1,0:T(8,128)S(1)}, f32[4,4,128,256]{3,2,1,0:T(8,128)}, u32[]{:S(2)}) copy-start(f32[4,4,128,256]{3,2,1,0:T(8,128)} %get-tuple-element.5) | copy-start | bytes 6291460

commit v2 on v1

v2 whole, which is shorter than its diff:
```python
import jax
import jax.numpy as jnp
import numpy as np
from jax import lax
from jax.experimental import pallas as pl
from jax.experimental.pallas import tpu as pltpu
from jax.sharding import PartitionSpec as P

MESH = pl.DeviceIdType.MESH
N = 256
FIELDS = 4
HIGHEST = lax.Precision.HIGHEST
F32 = jnp.float32


def dft_blocks():
    steps = np.outer(np.arange(N), np.arange(N)) % N
    angles = steps * (2.0 * np.pi / N)
    cos_part, sin_part = np.cos(angles) / np.sqrt(N), np.sin(angles) / np.sqrt(N)
    real_rows = np.stack([cos_part, sin_part], axis=1)
    imag_rows = np.stack([-sin_part, cos_part], axis=1)
    return np.stack([real_rows, imag_rows])


def matrices():
    full = dft_blocks()
    x_mat = full.reshape(2, 64, 4, 2, N).transpose(1, 0, 2, 3, 4).reshape(512, 512)
    y_mat = full.reshape(2, 2, 128, 2, 64, 4).transpose(1, 0, 2, 3, 5, 4).reshape(512, 512)
    z_mat = full.transpose(2, 3, 0, 1).reshape(512, 512)
    return [m.astype(np.float32) for m in (x_mat, y_mat, z_mat)]


STREAMS = ((2, 1, 0), (1, 0, 2), (0, 2, 1))


def kernel(ur_hbm, ui_hbm, g_hbm, xm_hbm, ym_hbm, zm_hbm, wr_hbm, wi_hbm,
           u_buf, xm, ym, zm, g_buf, cols, send, hop1, hop2, recv, planes, ysend, zbuf, wbuf,
           in_sem, send_sem, recv_sem, pair_send, pair_recv, out_sem):
    row, col = lax.axis_index("row"), lax.axis_index("col")
    other = 1 - col
    coord = (row // 16, (row // 4) % 4, row % 4)
    stride = (16, 4, 1)

    def mate(dim, step):
        there = (coord[dim] + step) % 4
        return there, row + (there - coord[dim]) * stride[dim]

    barrier = pltpu.get_barrier_semaphore()
    pl.semaphore_signal(barrier, 1, device_id=(0, other, row), device_id_type=MESH)
    for step in (1, 3, 2):
        for dim in range(3):
            pl.semaphore_signal(barrier, 1, device_id=(0, col, mate(dim, step)[1]), device_id_type=MESH)

    def load_u(f, part):
        src = (ur_hbm, ui_hbm)[part]
        return pltpu.make_async_copy(src.at[f], u_buf.at[f, part], in_sem.at[2 * f + part])

    x_load = pltpu.make_async_copy(xm_hbm, xm, in_sem.at[8])
    y_load = pltpu.make_async_copy(ym_hbm, ym, in_sem.at[9])
    z_load = pltpu.make_async_copy(zm_hbm, zm, in_sem.at[10])
    g_load = pltpu.make_async_copy(g_hbm, g_buf, in_sem.at[11])
    load_u(0, 0).start()
    load_u(0, 1).start()
    x_load.start()
    for f in range(1, FIELDS):
        load_u(f, 0).start()
        load_u(f, 1).start()
    y_load.start()
    z_load.start()
    g_load.start()
    x_load.wait()

    def x_step(f):
        load_u(f, 0).wait()
        load_u(f, 1).wait()

        @pl.loop(0, 2)
        def _(half):
            for part in range(2):
                for k in range(2):
                    cols[pl.ds(part * 256, 256), pl.ds(k * 128, 128)] = u_buf[f, part, pl.ds(2 * half + k, 256, stride=4), :]
            out = jnp.dot(xm[...], cols[...], precision=HIGHEST, preferred_element_type=F32)
            for k in range(2):
                send[f, 2 * half + k] = out[:, k * 128 : k * 128 + 128].reshape(4, 4, 4, 8, 128)

    bufs = (send, hop1, hop2, recv)

    def line(ref, f, yy, dim, at):
        where = [slice(None)] * 3
        where[dim] = at
        return ref.at[(f, yy, *where)]

    def forward(f, phase):
        cur, nxt = bufs[phase], bufs[phase + 1]

        def unit(yy, stream):
            dim = STREAMS[stream][phase]
            for step in (1, 3, 2):
                there, to = mate(dim, step)
                pltpu.make_async_remote_copy(
                    src_ref=line(cur, f, yy, dim, there),
                    dst_ref=line(nxt, f, yy, dim, coord[dim]),
                    send_sem=send_sem.at[phase, f, yy],
                    recv_sem=recv_sem.at[phase, f, yy],
                    device_id=(0, col, to),
                    device_id_type=MESH,
                ).start()
            line(nxt, f, yy, dim, coord[dim])[...] = line(cur, f, yy, dim, coord[dim])[...]

        for yy in range(3):
            unit(yy, yy)
        for stream in range(3):

            @pl.when(f % 3 == stream)
            def _():
                unit(3, stream)

    def arrived(f, phase):
        for yy in range(4):
            three = bufs[phase + 1].at[f, yy, pl.ds(0, 3)]
            pltpu.make_async_copy(three, three, recv_sem.at[phase, f, yy]).wait()

    def pair_copy(f, p):
        return pltpu.make_async_remote_copy(
            src_ref=ysend.at[f, p],
            dst_ref=zbuf.at[f, p, col],
            send_sem=pair_send.at[2 * f + p],
            recv_sem=pair_recv.at[2 * f + p],
            device_id=(0, other, row),
            device_id_type=MESH,
        )

    def y_step(f):
        @pl.loop(0, 2)
        def _(p):
            for yy in range(4):
                rows = recv.at[f, yy].reshape(512, 128)
                for part in range(2):
                    for k in range(2):
                        planes[pl.ds(part * 256 + yy * 64, 64), pl.ds(k * 128, 128)] = rows[pl.ds(part * 4 + 2 * p + k, 64, stride=8), :]
            theirs = jnp.dot(ym[pl.ds(pl.multiple_of(other * 256, 256), 256), :], planes[...], precision=HIGHEST, preferred_element_type=F32)
            for part in range(2):
                for k in range(2):
                    ysend[f, p, part, pl.ds(k * 128, 128), :] = theirs[part * 128 : part * 128 + 128, k * 128 : k * 128 + 128]
            pair_copy(f, p).start()
            ours = jnp.dot(ym[pl.ds(pl.multiple_of(col * 256, 256), 256), :], planes[...], precision=HIGHEST, preferred_element_type=F32)
            for part in range(2):
                for k in range(2):
                    zbuf[f, p, col, part, pl.ds(k * 128, 128), :] = ours[part * 128 : part * 128 + 128, k * 128 : k * 128 + 128]

    def out_copies(f, p):
        return [
            pltpu.make_async_copy(wbuf.at[f, part, pl.ds(2 * p, 2)], (wr_hbm, wi_hbm)[part].at[f, pl.ds(2 * p, 2)], out_sem.at[2 * f + p, part])
            for part in range(2)
        ]

    def z_step(f):
        @pl.loop(0, 2)
        def _(p):
            pair_copy(f, p).wait_recv()
            lines = jnp.concatenate([zbuf[f, p, h, part] for part in range(2) for h in range(2)], axis=1)
            out = jnp.dot(lines, zm[...], precision=HIGHEST, preferred_element_type=F32)
            for part in range(2):
                for k in range(2):
                    wbuf[f, part, 2 * p + k] = out[k * 128 : k * 128 + 128, part * 256 : part * 256 + 256] * g_buf[2 * p + k]
            for copy in out_copies(f, p):
                copy.start()

    @pl.loop(0, FIELDS + 4)
    def _(t):
        @pl.when(t < FIELDS)
        def _():
            x_step(t)

            @pl.when(t == 0)
            def _():
                pl.semaphore_wait(barrier, 10)

            forward(t, 0)

        for phase in (1, 2):

            @pl.when((t >= phase) & (t < FIELDS + phase))
            def _():
                arrived(t - phase, phase - 1)
                forward(t - phase, phase)

        @pl.when(t == 3)
        def _():
            y_load.wait()
            z_load.wait()
            g_load.wait()

        @pl.when(t >= 4)
        def _():
            z_step(t - 4)

        @pl.when((t >= 3) & (t < FIELDS + 3))
        def _():
            arrived(t - 3, 2)
            y_step(t - 3)

    @pl.loop(0, FIELDS)
    def _(f):
        for phase in range(3):
            for yy in range(4):
                three = bufs[phase].at[f, yy, pl.ds(0, 3)]
                pltpu.make_async_copy(three, three, send_sem.at[phase, f, yy]).wait()
        for p in range(2):
            pair_copy(f, p).wait_send()
            for copy in out_copies(f, p):
                copy.wait()


def solution(mesh):
    mats = matrices()

    def local_forward(u_real, u_imag, g_filter):
        flat = (FIELDS, 4 * N, 128)
        hbm_spec = pl.BlockSpec(memory_space=pltpu.HBM)
        out = jax.ShapeDtypeStruct((FIELDS, 4, 128, N), F32)
        return pl.pallas_call(
            kernel,
            out_shape=(out, out),
            in_specs=[hbm_spec] * 6,
            out_specs=(hbm_spec, hbm_spec),
            scratch_shapes=[
                pltpu.VMEM((FIELDS, 2, 4 * N, 128), F32),
                pltpu.VMEM((512, 512), F32),
                pltpu.VMEM((512, 512), F32),
                pltpu.VMEM((512, 512), F32),
                pltpu.VMEM((4, 128, N), F32),
                pltpu.VMEM((512, 256), F32),
                *[pltpu.VMEM((FIELDS, 4, 4, 4, 4, 8, 128), F32)] * 4,
                pltpu.VMEM((512, 256), F32),
                pltpu.VMEM((FIELDS, 2, 2, 256, 128), F32),
                pltpu.VMEM((FIELDS, 2, 2, 2, 256, 128), F32),
                pltpu.VMEM((FIELDS, 2, 4, 128, N), F32),
                pltpu.SemaphoreType.DMA((12,)),
                pltpu.SemaphoreType.DMA((3, FIELDS, 4)),
                pltpu.SemaphoreType.DMA((3, FIELDS, 4)),
                pltpu.SemaphoreType.DMA((2 * FIELDS,)),
                pltpu.SemaphoreType.DMA((2 * FIELDS,)),
                pltpu.SemaphoreType.DMA((2 * FIELDS, 2)),
            ],
            compiler_params=pltpu.CompilerParams(collective_id=0, has_side_effects=True, vmem_limit_bytes=56 * 2**20),
        )(u_real.reshape(flat), u_imag.reshape(flat), g_filter, *[jnp.asarray(m) for m in mats])

    field_spec = P("fld", None, "row", "col")
    out_spec = P("fld", "row", "col", None)
    return jax.shard_map(local_forward, mesh=mesh, in_specs=(field_spec, field_spec, P("row", "col", None)), out_specs=(out_spec, out_spec), check_vma=False)
```

time: 84.7 us -> 76.5 us (0.903)
  Pallas kernels: 79.4 us -> 71.2 us
    pallas_call x1, Pallas kernels: 79.4 us -> 71.2 us  [local_forward(): pl.pallas_call(kernel, out_shape=(out, out), in_specs=[hbm_spec] * 6, out...]
where the time goes in v2:
time: 76.5 us; the launch traced here: 76.4 us
  Pallas kernels  71.2 us (93%)
  local copies, waits for them, and re-layouts  4.57 us (6%)
    pallas_call x1, Pallas kernels, local_forward(): pl.pallas_call(kernel, out_shape=(out, out), in_specs=[hbm_spec] * 6, out...  71.2 us
    unnamed x4, local copies, waits for them, and re-layouts  4.57 us

profile of v2, /device:TPU:1, one launch (start us, length us, event | category | flops | bytes accessed | tf_op | source)
XLA Modules:
  0.0 76.4 jit_solution(9967317934050051807)
XLA Ops:
  0.6 71.2 %shard_map.77 = (f32[4,4,128,256]{3,2,1,0:T(8,128)}, f32[4,4,128,256]{3,2,1,0:T(8,128)}) custom-call(f32[4,1024,128]{2,1,0:T(8,128)} %bitcast.2, f32[4,1024,128]{2,1,0:T(8,128)} %bitcast.3, f32[4,128,256]{2,1,0:T(8,128)} %g_hbm.1, f32[512,512]{1,0:T(8,128)} %constant.6.clone.xm_hbm, f32[512,512]{1,0:T(8,128)} %constant.7.clone.ym_hbm, ...), custom_call_target="tpu_custom_call" | custom-call | tf_op jit(solution)/shard_map/pallas_call | solution.py:222
  71.8 0.0 copy-start
  71.8 3.2 %copy.10 = f32[4,4,128,256]{3,2,1,0:T(8,128)} copy(f32[4,4,128,256]{3,2,1,0:T(8,128)} %get-tuple-element.4) | data formatting | bytes 4194304
  75.1 0.0 copy-done
  75.1 1.3 %copy.11 = f32[4,4,128,256]{3,2,1,0:T(8,128)} copy(f32[4,4,128,256]{3,2,1,0:T(8,128)S(1)} %copy-done) | data formatting | bytes 4194304
Async XLA Ops:
  71.8 3.3 %copy-start = (f32[4,4,128,256]{3,2,1,0:T(8,128)S(1)}, f32[4,4,128,256]{3,2,1,0:T(8,128)}, u32[]{:S(2)}) copy-start(f32[4,4,128,256]{3,2,1,0:T(8,128)} %get-tuple-element.5) | copy-start | bytes 6291460

commit v3 on v2

--- a/solution.py
+++ b/solution.py
@@ -33,9 +33,40 @@
 STREAMS = ((2, 1, 0), (1, 0, 2), (0, 2, 1))
 
 
-def kernel(ur_hbm, ui_hbm, g_hbm, xm_hbm, ym_hbm, zm_hbm, wr_hbm, wi_hbm,
-           u_buf, xm, ym, zm, g_buf, cols, send, hop1, hop2, recv, planes, ysend, zbuf, wbuf,
-           in_sem, send_sem, recv_sem, pair_send, pair_recv, out_sem):
+def z_product(zbuf, zm, g_buf, f, p):
+    lines = jnp.concatenate([zbuf[f, p, h, part] for part in range(2) for h in range(2)], axis=1)
+    out = jnp.dot(lines, zm[...], precision=HIGHEST, preferred_element_type=F32)
+    return {
+        (part, k): out[k * 128 : k * 128 + 128, part * 256 : part * 256 + 256] * g_buf[2 * p + k]
+        for part in range(2)
+        for k in range(2)
+    }
+
+
+def last_kernel(zbuf, wbuf, zm, g_buf, wr_hbm, wi_hbm, w_last, out_sem, last_sem):
+    outs = (wr_hbm, wi_hbm)
+    done = [
+        pltpu.make_async_copy(wbuf.at[f, part], outs[part].at[f], out_sem.at[2 * f + part])
+        for f in range(FIELDS - 1)
+        for part in range(2)
+    ]
+    for copy in done:
+        copy.start()
+    last = FIELDS - 1
+    for p in range(2):
+        for (part, k), value in z_product(zbuf, zm, g_buf, last, p).items():
+            w_last[part, 2 * p + k] = value
+        for part in range(2):
+            copy = pltpu.make_async_copy(w_last.at[part, pl.ds(2 * p, 2)], outs[part].at[last, pl.ds(2 * p, 2)], last_sem.at[2 * p + part])
+            copy.start()
+            done.append(copy)
+    for copy in done:
+        copy.wait()
+
+
+def kernel(ur_hbm, ui_hbm, g_hbm, xm_hbm, ym_hbm, zm_hbm, zbuf, wbuf, zm, g_buf,
+           u_buf, xm, ym, cols, send, hop1, hop2, recv, planes, ysend,
+           in_sem, send_sem, recv_sem, pair_send, pair_recv):
     row, col = lax.axis_index("row"), lax.axis_index("col")
     other = 1 - col
     coord = (row // 16, (row // 4) % 4, row % 4)
@@ -90,11 +121,17 @@
         where[dim] = at
         return ref.at[(f, yy, *where)]
 
+    def arrived(f, phase, yy):
+        three = bufs[phase + 1].at[f, yy, pl.ds(0, 3)]
+        pltpu.make_async_copy(three, three, recv_sem.at[phase, f, yy]).wait()
+
     def forward(f, phase):
         cur, nxt = bufs[phase], bufs[phase + 1]
 
         def unit(yy, stream):
             dim = STREAMS[stream][phase]
+            if phase:
+                arrived(f, phase - 1, yy)
             for step in (1, 3, 2):
                 there, to = mate(dim, step)
                 pltpu.make_async_remote_copy(
@@ -114,11 +151,6 @@
             @pl.when(f % 3 == stream)
             def _():
                 unit(3, stream)
-
-    def arrived(f, phase):
-        for yy in range(4):
-            three = bufs[phase + 1].at[f, yy, pl.ds(0, 3)]
-            pltpu.make_async_copy(three, three, recv_sem.at[phase, f, yy]).wait()
 
     def pair_copy(f, p):
         return pltpu.make_async_remote_copy(
@@ -142,29 +174,18 @@
             for part in range(2):
                 for k in range(2):
                     ysend[f, p, part, pl.ds(k * 128, 128), :] = theirs[part * 128 : part * 128 + 128, k * 128 : k * 128 + 128]
-            pair_copy(f, p).start()
             ours = jnp.dot(ym[pl.ds(pl.multiple_of(col * 256, 256), 256), :], planes[...], precision=HIGHEST, preferred_element_type=F32)
             for part in range(2):
                 for k in range(2):
                     zbuf[f, p, col, part, pl.ds(k * 128, 128), :] = ours[part * 128 : part * 128 + 128, k * 128 : k * 128 + 128]
-
-    def out_copies(f, p):
-        return [
-            pltpu.make_async_copy(wbuf.at[f, part, pl.ds(2 * p, 2)], (wr_hbm, wi_hbm)[part].at[f, pl.ds(2 * p, 2)], out_sem.at[2 * f + p, part])
-            for part in range(2)
-        ]
+            pair_copy(f, p).start()
 
     def z_step(f):
         @pl.loop(0, 2)
         def _(p):
             pair_copy(f, p).wait_recv()
-            lines = jnp.concatenate([zbuf[f, p, h, part] for part in range(2) for h in range(2)], axis=1)
-            out = jnp.dot(lines, zm[...], precision=HIGHEST, preferred_element_type=F32)
-            for part in range(2):
-                for k in range(2):
-                    wbuf[f, part, 2 * p + k] = out[k * 128 : k * 128 + 128, part * 256 : part * 256 + 256] * g_buf[2 * p + k]
-            for copy in out_copies(f, p):
-                copy.start()
+            for (part, k), value in z_product(zbuf, zm, g_buf, f, p).items():
+                wbuf[f, part, 2 * p + k] = value
 
     @pl.loop(0, FIELDS + 4)
     def _(t):
@@ -180,10 +201,9 @@
 
         for phase in (1, 2):
 
-            @pl.when((t >= phase) & (t < FIELDS + phase))
+            @pl.when((t > phase) & (t <= FIELDS + phase))
             def _():
-                arrived(t - phase, phase - 1)
-                forward(t - phase, phase)
+                forward(t - phase - 1, phase)
 
         @pl.when(t == 3)
         def _():
@@ -191,14 +211,18 @@
             z_load.wait()
             g_load.wait()
 
-        @pl.when(t >= 4)
-        def _():
-            z_step(t - 4)
-
-        @pl.when((t >= 3) & (t < FIELDS + 3))
-        def _():
-            arrived(t - 3, 2)
-            y_step(t - 3)
+        @pl.when(t >= 5)
+        def _():
+            z_step(t - 5)
+
+        @pl.when((t >= 4) & (t < FIELDS + 4))
+        def _():
+            for yy in range(4):
+                arrived(t - 4, 2, yy)
+            y_step(t - 4)
+
+    for p in range(2):
+        pair_copy(FIELDS - 1, p).wait_recv()
 
     @pl.loop(0, FIELDS)
     def _(f):
@@ -208,8 +232,6 @@
                 pltpu.make_async_copy(three, three, send_sem.at[phase, f, yy]).wait()
         for p in range(2):
             pair_copy(f, p).wait_send()
-            for copy in out_copies(f, p):
-                copy.wait()
 
 
 def solution(mesh):
@@ -218,33 +240,46 @@
     def local_forward(u_real, u_imag, g_filter):
         flat = (FIELDS, 4 * N, 128)
         hbm_spec = pl.BlockSpec(memory_space=pltpu.HBM)
-        out = jax.ShapeDtypeStruct((FIELDS, 4, 128, N), F32)
-        return pl.pallas_call(
+        vmem_spec = pl.BlockSpec(memory_space=pltpu.VMEM)
+        kept = pl.pallas_call(
             kernel,
-            out_shape=(out, out),
+            out_shape=(
+                pltpu.VMEM((FIELDS, 2, 2, 2, 256, 128), F32),
+                pltpu.VMEM((FIELDS - 1, 2, 4, 128, N), F32),
+                pltpu.VMEM((512, 512), F32),
+                pltpu.VMEM((4, 128, N), F32),
+            ),
             in_specs=[hbm_spec] * 6,
-            out_specs=(hbm_spec, hbm_spec),
+            out_specs=(vmem_spec,) * 4,
             scratch_shapes=[
                 pltpu.VMEM((FIELDS, 2, 4 * N, 128), F32),
                 pltpu.VMEM((512, 512), F32),
                 pltpu.VMEM((512, 512), F32),
-                pltpu.VMEM((512, 512), F32),
-                pltpu.VMEM((4, 128, N), F32),
                 pltpu.VMEM((512, 256), F32),
                 *[pltpu.VMEM((FIELDS, 4, 4, 4, 4, 8, 128), F32)] * 4,
                 pltpu.VMEM((512, 256), F32),
                 pltpu.VMEM((FIELDS, 2, 2, 256, 128), F32),
-                pltpu.VMEM((FIELDS, 2, 2, 2, 256, 128), F32),
-                pltpu.VMEM((FIELDS, 2, 4, 128, N), F32),
                 pltpu.SemaphoreType.DMA((12,)),
                 pltpu.SemaphoreType.DMA((3, FIELDS, 4)),
                 pltpu.SemaphoreType.DMA((3, FIELDS, 4)),
                 pltpu.SemaphoreType.DMA((2 * FIELDS,)),
                 pltpu.SemaphoreType.DMA((2 * FIELDS,)),
-                pltpu.SemaphoreType.DMA((2 * FIELDS, 2)),
             ],
-            compiler_params=pltpu.CompilerParams(collective_id=0, has_side_effects=True, vmem_limit_bytes=56 * 2**20),
+            compiler_params=pltpu.CompilerParams(collective_id=0, has_side_effects=True, vmem_limit_bytes=55 * 2**20),
         )(u_real.reshape(flat), u_imag.reshape(flat), g_filter, *[jnp.asarray(m) for m in mats])
+        out = jax.ShapeDtypeStruct((FIELDS, 4, 128, N), F32)
+        return pl.pallas_call(
+            last_kernel,
+            out_shape=(out, out),
+            in_specs=[vmem_spec] * 4,
+            out_specs=(hbm_spec, hbm_spec),
+            scratch_shapes=[
+                pltpu.VMEM((2, 4, 128, N), F32),
+                pltpu.SemaphoreType.DMA((2 * FIELDS - 2,)),
+                pltpu.SemaphoreType.DMA((4,)),
+            ],
+            compiler_params=pltpu.CompilerParams(vmem_limit_bytes=40 * 2**20),
+        )(*kept)
 
     field_spec = P("fld", None, "row", "col")
     out_spec = P("fld", "row", "col", None)

time: 76.5 us -> 69.1 us (0.903)
  local copies, waits for them, and re-layouts: 4.57 us -> 0 us
  Pallas kernels: 71.2 us -> 68.4 us
    unnamed x4 -> x0, local copies, waits for them, and re-layouts: 4.57 us -> none
    pallas_call x1 -> x2, Pallas kernels: 71.2 us -> 68.4 us  [the longest x1 65.5 us: local_forward(): pl.pallas_call(kernel, out_shape=(pltpu.VMEM((FIELDS, 2, 2, 2, 256, 128),...]
where the time goes in v3:
time: 69.1 us; the launch traced here: 69 us
  Pallas kernels  68.4 us (99%)
    pallas_call x1, Pallas kernels, local_forward(): pl.pallas_call(kernel, out_shape=(pltpu.VMEM((FIELDS, 2, 2, 2, 256, 128),...  65.5 us
    pallas_call x1, Pallas kernels, local_forward(): pl.pallas_call(last_kernel, out_shape=(out, out), in_specs=[vmem_spec] *...  2.83 us

profile of v3, /device:TPU:1, one launch (start us, length us, event | category | flops | bytes accessed | tf_op | source)
XLA Modules:
  0.0 69.0 jit_solution(6783774822204966258)
XLA Ops:
  0.6 65.5 %shard_map.77 = (f32[4,2,2,2,256,128]{5,4,3,2,1,0:T(8,128)S(1)}, f32[3,2,4,128,256]{4,3,2,1,0:T(8,128)S(1)}, f32[512,512]{1,0:T(8,128)S(1)}, f32[4,128,256]{2,1,0:T(8,128)S(1)}) custom-call(f32[4,1024,128]{2,1,0:T(8,128)} %bitcast.2, f32[4,1024,128]{2,1,0:T(8,128)} %bitcast.3, f32[4,128,256]{2,1,0:T(8,128)} %g_hbm.1, f32[512,512]{1,0:T(8,128)} %constant.6.clone.xm_hbm, ...), custom_call_target="tpu_custom_call" | custom-call | tf_op jit(solution)/shard_map/pallas_call | solution.py:244
  66.2 2.8 %shard_map.78 = (f32[4,4,128,256]{3,2,1,0:T(8,128)}, f32[4,4,128,256]{3,2,1,0:T(8,128)}) custom-call(f32[4,2,2,2,256,128]{5,4,3,2,1,0:T(8,128)S(1)} %get-tuple-element.6.zbuf, f32[3,2,4,128,256]{4,3,2,1,0:T(8,128)S(1)} %get-tuple-element.7.wbuf, f32[512,512]{1,0:T(8,128)S(1)} %get-tuple-element.8.zm, f32[4,128,256]{2,1,0:T(8,128)S(1)} %get-tuple-element.9.g_buf), custom_call_target="tpu_custom_call" | custom-call | tf_op jit(solution)/shard_map/pallas_call | solution.py:271

commit v4 on v3

--- a/solution.py
+++ b/solution.py
@@ -187,7 +187,7 @@
             for (part, k), value in z_product(zbuf, zm, g_buf, f, p).items():
                 wbuf[f, part, 2 * p + k] = value
 
-    @pl.loop(0, FIELDS + 4)
+    @pl.loop(0, FIELDS + 6)
     def _(t):
         @pl.when(t < FIELDS)
         def _():
@@ -201,26 +201,27 @@
 
         for phase in (1, 2):
 
-            @pl.when((t > phase) & (t <= FIELDS + phase))
+            @pl.when((t >= 2 * phase) & (t < FIELDS + 2 * phase))
             def _():
-                forward(t - phase - 1, phase)
-
-        @pl.when(t == 3)
+                forward(t - 2 * phase, phase)
+
+        @pl.when(t == 6)
         def _():
             y_load.wait()
             z_load.wait()
             g_load.wait()
 
-        @pl.when(t >= 5)
-        def _():
-            z_step(t - 5)
-
-        @pl.when((t >= 4) & (t < FIELDS + 4))
+        @pl.when((t == 7) | (t == 8))
+        def _():
+            z_step(t - 7)
+
+        @pl.when(t >= 6)
         def _():
             for yy in range(4):
-                arrived(t - 4, 2, yy)
-            y_step(t - 4)
-
+                arrived(t - 6, 2, yy)
+            y_step(t - 6)
+
+    z_step(FIELDS - 2)
     for p in range(2):
         pair_copy(FIELDS - 1, p).wait_recv()
 

time: 69.1 us -> 65 us (0.941)
  Pallas kernels: 68.4 us -> 64.3 us
    pallas_call x1, Pallas kernels: 65.5 us -> 61.4 us  [local_forward(): pl.pallas_call(kernel, out_shape=(pltpu.VMEM((FIELDS, 2, 2, 2, 256, 128),...]
where the time goes in v4:
time: 65 us; the launch traced here: 64.9 us
  Pallas kernels  64.3 us (99%)
    pallas_call x1, Pallas kernels, local_forward(): pl.pallas_call(kernel, out_shape=(pltpu.VMEM((FIELDS, 2, 2, 2, 256, 128),...  61.4 us
    pallas_call x1, Pallas kernels, local_forward(): pl.pallas_call(last_kernel, out_shape=(out, out), in_specs=[vmem_spec] *...  2.83 us

profile of v4, /device:TPU:1, one launch (start us, length us, event | category | flops | bytes accessed | tf_op | source)
XLA Modules:
  0.0 64.9 jit_solution(6956722488099347210)
XLA Ops:
  0.6 61.4 %shard_map.77 = (f32[4,2,2,2,256,128]{5,4,3,2,1,0:T(8,128)S(1)}, f32[3,2,4,128,256]{4,3,2,1,0:T(8,128)S(1)}, f32[512,512]{1,0:T(8,128)S(1)}, f32[4,128,256]{2,1,0:T(8,128)S(1)}) custom-call(f32[4,1024,128]{2,1,0:T(8,128)} %bitcast.2, f32[4,1024,128]{2,1,0:T(8,128)} %bitcast.3, f32[4,128,256]{2,1,0:T(8,128)} %g_hbm.1, f32[512,512]{1,0:T(8,128)} %constant.6.clone.xm_hbm, ...), custom_call_target="tpu_custom_call" | custom-call | tf_op jit(solution)/shard_map/pallas_call | solution.py:245
  62.1 2.8 %shard_map.78 = (f32[4,4,128,256]{3,2,1,0:T(8,128)}, f32[4,4,128,256]{3,2,1,0:T(8,128)}) custom-call(f32[4,2,2,2,256,128]{5,4,3,2,1,0:T(8,128)S(1)} %get-tuple-element.6.zbuf, f32[3,2,4,128,256]{4,3,2,1,0:T(8,128)S(1)} %get-tuple-element.7.wbuf, f32[512,512]{1,0:T(8,128)S(1)} %get-tuple-element.8.zm, f32[4,128,256]{2,1,0:T(8,128)S(1)} %get-tuple-element.9.g_buf), custom_call_target="tpu_custom_call" | custom-call | tf_op jit(solution)/shard_map/pallas_call | solution.py:272

commit v5 on v4

--- a/solution.py
+++ b/solution.py
@@ -9,25 +9,37 @@
 MESH = pl.DeviceIdType.MESH
 N = 256
 FIELDS = 4
+SCALE = 1.0 / 16.0
 HIGHEST = lax.Precision.HIGHEST
 F32 = jnp.float32
 
 
-def dft_blocks():
-    steps = np.outer(np.arange(N), np.arange(N)) % N
-    angles = steps * (2.0 * np.pi / N)
-    cos_part, sin_part = np.cos(angles) / np.sqrt(N), np.sin(angles) / np.sqrt(N)
+def dft_blocks(length):
+    steps = np.outer(np.arange(length), np.arange(length)) % length
+    angles = steps * (2.0 * np.pi / length)
+    cos_part, sin_part = np.cos(angles), np.sin(angles)
     real_rows = np.stack([cos_part, sin_part], axis=1)
     imag_rows = np.stack([-sin_part, cos_part], axis=1)
     return np.stack([real_rows, imag_rows])
 
 
 def matrices():
-    full = dft_blocks()
-    x_mat = full.reshape(2, 64, 4, 2, N).transpose(1, 0, 2, 3, 4).reshape(512, 512)
-    y_mat = full.reshape(2, 2, 128, 2, 64, 4).transpose(1, 0, 2, 3, 5, 4).reshape(512, 512)
+    half, full = dft_blocks(N // 2), dft_blocks(N) * SCALE
+    x_mat = half.reshape(2, 64, 2, 2, 128).transpose(1, 0, 2, 3, 4).reshape(256, 256)
+    y_mat = half.reshape(2, 2, 64, 2, 32, 4).transpose(1, 0, 2, 3, 5, 4).reshape(256, 256)
     z_mat = full.transpose(2, 3, 0, 1).reshape(512, 512)
-    return [m.astype(np.float32) for m in (x_mat, y_mat, z_mat)]
+    turns = np.arange(N // 2) * (2.0 * np.pi / N)
+    y_turns = turns.reshape(32, 4).T.reshape(-1)
+    factors = np.stack([np.cos(turns), np.sin(turns), np.cos(y_turns), np.sin(y_turns)])
+    factors = np.repeat(factors[:, :, None], 128, axis=2)
+    return [m.astype(np.float32) for m in (x_mat, y_mat, z_mat, factors)]
+
+
+def even_odd(low, high, cos, sin):
+    low, high = [v * SCALE for v in low], [v * SCALE for v in high]
+    even = [a + b for a, b in zip(low, high)]
+    re, im = [a - b for a, b in zip(low, high)]
+    return even, [re * cos + im * sin, im * cos - re * sin]
 
 
 STREAMS = ((2, 1, 0), (1, 0, 2), (0, 2, 1))
@@ -64,8 +76,8 @@
         copy.wait()
 
 
-def kernel(ur_hbm, ui_hbm, g_hbm, xm_hbm, ym_hbm, zm_hbm, zbuf, wbuf, zm, g_buf,
-           u_buf, xm, ym, cols, send, hop1, hop2, recv, planes, ysend,
+def kernel(ur_hbm, ui_hbm, g_hbm, xm_hbm, ym_hbm, zm_hbm, factor_hbm, zbuf, wbuf, zm, g_buf,
+           u_buf, xm, ym, factor, cols, send, hop1, hop2, recv, planes, ysend,
            in_sem, send_sem, recv_sem, pair_send, pair_recv):
     row, col = lax.axis_index("row"), lax.axis_index("col")
     other = 1 - col
@@ -87,19 +99,26 @@
         return pltpu.make_async_copy(src.at[f], u_buf.at[f, part], in_sem.at[2 * f + part])
 
     x_load = pltpu.make_async_copy(xm_hbm, xm, in_sem.at[8])
-    y_load = pltpu.make_async_copy(ym_hbm, ym, in_sem.at[9])
+    factor_load = pltpu.make_async_copy(factor_hbm, factor, in_sem.at[13])
+    y_loads = [
+        pltpu.make_async_copy(ym_hbm.at[pl.ds(pl.multiple_of(h * 128, 128), 128), :], ym.at[pl.ds(128 * place, 128), :], in_sem.at[sem])
+        for place, h, sem in ((0, other, 9), (1, col, 12))
+    ]
     z_load = pltpu.make_async_copy(zm_hbm, zm, in_sem.at[10])
     g_load = pltpu.make_async_copy(g_hbm, g_buf, in_sem.at[11])
     load_u(0, 0).start()
     load_u(0, 1).start()
     x_load.start()
+    factor_load.start()
     for f in range(1, FIELDS):
         load_u(f, 0).start()
         load_u(f, 1).start()
-    y_load.start()
+    for load in y_loads:
+        load.start()
     z_load.start()
     g_load.start()
     x_load.wait()
+    factor_load.wait()
 
     def x_step(f):
         load_u(f, 0).wait()
@@ -107,12 +126,19 @@
 
         @pl.loop(0, 2)
         def _(half):
-            for part in range(2):
-                for k in range(2):
-                    cols[pl.ds(part * 256, 256), pl.ds(k * 128, 128)] = u_buf[f, part, pl.ds(2 * half + k, 256, stride=4), :]
+            for k in range(2):
+                low, high = [
+                    [u_buf[f, part, pl.ds(first + 2 * half + k, 128, stride=4), :] for part in range(2)]
+                    for first in (0, 512)
+                ]
+                for parity, pair in enumerate(even_odd(low, high, factor[0], factor[1])):
+                    for part in range(2):
+                        cols[pl.ds(part * 128, 128), pl.ds((2 * k + parity) * 128, 128)] = pair[part]
             out = jnp.dot(xm[...], cols[...], precision=HIGHEST, preferred_element_type=F32)
             for k in range(2):
-                send[f, 2 * half + k] = out[:, k * 128 : k * 128 + 128].reshape(4, 4, 4, 8, 128)
+                rows = send.at[f, 2 * half + k].reshape(512, 128)
+                for parity in range(2):
+                    rows[pl.ds(parity, 256, stride=2), :] = out[:, (2 * k + parity) * 128 : (2 * k + parity) * 128 + 128]
 
     bufs = (send, hop1, hop2, recv)
 
@@ -167,17 +193,23 @@
         def _(p):
             for yy in range(4):
                 rows = recv.at[f, yy].reshape(512, 128)
-                for part in range(2):
-                    for k in range(2):
-                        planes[pl.ds(part * 256 + yy * 64, 64), pl.ds(k * 128, 128)] = rows[pl.ds(part * 4 + 2 * p + k, 64, stride=8), :]
-            theirs = jnp.dot(ym[pl.ds(pl.multiple_of(other * 256, 256), 256), :], planes[...], precision=HIGHEST, preferred_element_type=F32)
+                turn = pl.ds(yy * 32, 32)
+                for k in range(2):
+                    low, high = [
+                        [rows[pl.ds(first + part * 4 + 2 * p + k, 32, stride=8), :] for part in range(2)]
+                        for first in (0, 256)
+                    ]
+                    for parity, pair in enumerate(even_odd(low, high, factor[2, turn, :], factor[3, turn, :])):
+                        for part in range(2):
+                            planes[pl.ds(part * 128 + yy * 32, 32), pl.ds((2 * k + parity) * 128, 128)] = pair[part]
+            out = jnp.dot(ym[...], planes[...], precision=HIGHEST, preferred_element_type=F32)
             for part in range(2):
                 for k in range(2):
-                    ysend[f, p, part, pl.ds(k * 128, 128), :] = theirs[part * 128 : part * 128 + 128, k * 128 : k * 128 + 128]
-            ours = jnp.dot(ym[pl.ds(pl.multiple_of(col * 256, 256), 256), :], planes[...], precision=HIGHEST, preferred_element_type=F32)
-            for part in range(2):
-                for k in range(2):
-                    zbuf[f, p, col, part, pl.ds(k * 128, 128), :] = ours[part * 128 : part * 128 + 128, k * 128 : k * 128 + 128]
+                    for parity in range(2):
+                        lanes = slice((2 * k + parity) * 128, (2 * k + parity) * 128 + 128)
+                        where = pl.ds(k * 128 + parity, 64, stride=2)
+                        ysend[f, p, part, where, :] = out[part * 64 : part * 64 + 64, lanes]
+                        zbuf[f, p, col, part, where, :] = out[128 + part * 64 : 128 + part * 64 + 64, lanes]
             pair_copy(f, p).start()
 
     def z_step(f):
@@ -207,7 +239,8 @@
 
         @pl.when(t == 6)
         def _():
-            y_load.wait()
+            for load in y_loads:
+                load.wait()
             z_load.wait()
             g_load.wait()
 
@@ -250,17 +283,18 @@
                 pltpu.VMEM((512, 512), F32),
                 pltpu.VMEM((4, 128, N), F32),
             ),
-            in_specs=[hbm_spec] * 6,
+            in_specs=[hbm_spec] * 7,
             out_specs=(vmem_spec,) * 4,
             scratch_shapes=[
                 pltpu.VMEM((FIELDS, 2, 4 * N, 128), F32),
-                pltpu.VMEM((512, 512), F32),
-                pltpu.VMEM((512, 512), F32),
-                pltpu.VMEM((512, 256), F32),
+                pltpu.VMEM((256, 256), F32),
+                pltpu.VMEM((256, 256), F32),
+                pltpu.VMEM((4, 128, 128), F32),
+                pltpu.VMEM((256, 512), F32),
                 *[pltpu.VMEM((FIELDS, 4, 4, 4, 4, 8, 128), F32)] * 4,
-                pltpu.VMEM((512, 256), F32),
+                pltpu.VMEM((256, 512), F32),
                 pltpu.VMEM((FIELDS, 2, 2, 256, 128), F32),
-                pltpu.SemaphoreType.DMA((12,)),
+                pltpu.SemaphoreType.DMA((14,)),
                 pltpu.SemaphoreType.DMA((3, FIELDS, 4)),
                 pltpu.SemaphoreType.DMA((3, FIELDS, 4)),
                 pltpu.SemaphoreType.DMA((2 * FIELDS,)),

time: 65 us -> 63.2 us (0.972)
  Pallas kernels: 64.3 us -> 62.5 us
    pallas_call x1, Pallas kernels: 61.4 us -> 59.7 us  [local_forward(): pl.pallas_call(kernel, out_shape=(pltpu.VMEM((FIELDS, 2, 2, 2, 256, 128),...]
where the time goes in v5:
time: 63.2 us; the launch traced here: 63.1 us
  Pallas kernels  62.5 us (99%)
  between operations  0.64 us (1%)
    pallas_call x1, Pallas kernels, local_forward(): pl.pallas_call(kernel, out_shape=(pltpu.VMEM((FIELDS, 2, 2, 2, 256, 128),...  59.7 us
    pallas_call x1, Pallas kernels, local_forward(): pl.pallas_call(last_kernel, out_shape=(out, out), in_specs=[vmem_spec] *...  2.83 us

profile of v5, /device:TPU:1, one launch (start us, length us, event | category | flops | bytes accessed | tf_op | source)
XLA Modules:
  0.0 63.1 jit_solution(18135625383194759266)
XLA Ops:
  0.6 59.7 %shard_map.86 = (f32[4,2,2,2,256,128]{5,4,3,2,1,0:T(8,128)S(1)}, f32[3,2,4,128,256]{4,3,2,1,0:T(8,128)S(1)}, f32[512,512]{1,0:T(8,128)S(1)}, f32[4,128,256]{2,1,0:T(8,128)S(1)}) custom-call(f32[4,1024,128]{2,1,0:T(8,128)} %bitcast.2, f32[4,1024,128]{2,1,0:T(8,128)} %bitcast.3, f32[4,128,256]{2,1,0:T(8,128)} %g_hbm.1, f32[256,256]{1,0:T(8,128)} %constant.8.clone.xm_hbm, ...), custom_call_target="tpu_custom_call" | custom-call | tf_op jit(solution)/shard_map/pallas_call | solution.py:278
  60.3 2.8 %shard_map.87 = (f32[4,4,128,256]{3,2,1,0:T(8,128)}, f32[4,4,128,256]{3,2,1,0:T(8,128)}) custom-call(f32[4,2,2,2,256,128]{5,4,3,2,1,0:T(8,128)S(1)} %get-tuple-element.6.zbuf, f32[3,2,4,128,256]{4,3,2,1,0:T(8,128)S(1)} %get-tuple-element.7.wbuf, f32[512,512]{1,0:T(8,128)S(1)} %get-tuple-element.8.zm, f32[4,128,256]{2,1,0:T(8,128)S(1)} %get-tuple-element.9.g_buf), custom_call_target="tpu_custom_call" | custom-call | tf_op jit(solution)/shard_map/pallas_call | solution.py:306

commit v6 on v5

--- a/solution.py
+++ b/solution.py
@@ -120,25 +120,20 @@
     x_load.wait()
     factor_load.wait()
 
-    def x_step(f):
-        load_u(f, 0).wait()
-        load_u(f, 1).wait()
-
-        @pl.loop(0, 2)
-        def _(half):
-            for k in range(2):
-                low, high = [
-                    [u_buf[f, part, pl.ds(first + 2 * half + k, 128, stride=4), :] for part in range(2)]
-                    for first in (0, 512)
-                ]
-                for parity, pair in enumerate(even_odd(low, high, factor[0], factor[1])):
-                    for part in range(2):
-                        cols[pl.ds(part * 128, 128), pl.ds((2 * k + parity) * 128, 128)] = pair[part]
-            out = jnp.dot(xm[...], cols[...], precision=HIGHEST, preferred_element_type=F32)
-            for k in range(2):
-                rows = send.at[f, 2 * half + k].reshape(512, 128)
-                for parity in range(2):
-                    rows[pl.ds(parity, 256, stride=2), :] = out[:, (2 * k + parity) * 128 : (2 * k + parity) * 128 + 128]
+    def x_step(f, half):
+        for k in range(2):
+            low, high = [
+                [u_buf[f, part, pl.ds(first + 2 * half + k, 128, stride=4), :] for part in range(2)]
+                for first in (0, 512)
+            ]
+            for parity, pair in enumerate(even_odd(low, high, factor[0], factor[1])):
+                for part in range(2):
+                    cols[half, pl.ds(part * 128, 128), pl.ds((2 * k + parity) * 128, 128)] = pair[part]
+        out = jnp.dot(xm[...], cols[half], precision=HIGHEST, preferred_element_type=F32)
+        for k in range(2):
+            rows = send.at[f, 2 * half + k].reshape(512, 128)
+            for parity in range(2):
+                rows[pl.ds(parity, 256, stride=2), :] = out[:, (2 * k + parity) * 128 : (2 * k + parity) * 128 + 128]
 
     bufs = (send, hop1, hop2, recv)
 
@@ -151,14 +146,14 @@
         three = bufs[phase + 1].at[f, yy, pl.ds(0, 3)]
         pltpu.make_async_copy(three, three, recv_sem.at[phase, f, yy]).wait()
 
-    def forward(f, phase):
+    def forward(f, phase, blocks=range(4)):
         cur, nxt = bufs[phase], bufs[phase + 1]
 
         def unit(yy, stream):
             dim = STREAMS[stream][phase]
             if phase:
                 arrived(f, phase - 1, yy)
-            for step in (1, 3, 2):
+            for step in (2, 1, 3):
                 there, to = mate(dim, step)
                 pltpu.make_async_remote_copy(
                     src_ref=line(cur, f, yy, dim, there),
@@ -170,9 +165,10 @@
                 ).start()
             line(nxt, f, yy, dim, coord[dim])[...] = line(cur, f, yy, dim, coord[dim])[...]
 
-        for yy in range(3):
-            unit(yy, yy)
-        for stream in range(3):
+        for yy in blocks:
+            if yy < 3:
+                unit(yy, yy)
+        for stream in range(3 if 3 in blocks else 0):
 
             @pl.when(f % 3 == stream)
             def _():
@@ -189,8 +185,7 @@
         )
 
     def y_step(f):
-        @pl.loop(0, 2)
-        def _(p):
+        for p in range(2):
             for yy in range(4):
                 rows = recv.at[f, yy].reshape(512, 128)
                 turn = pl.ds(yy * 32, 32)
@@ -201,8 +196,8 @@
                     ]
                     for parity, pair in enumerate(even_odd(low, high, factor[2, turn, :], factor[3, turn, :])):
                         for part in range(2):
-                            planes[pl.ds(part * 128 + yy * 32, 32), pl.ds((2 * k + parity) * 128, 128)] = pair[part]
-            out = jnp.dot(ym[...], planes[...], precision=HIGHEST, preferred_element_type=F32)
+                            planes[p, pl.ds(part * 128 + yy * 32, 32), pl.ds((2 * k + parity) * 128, 128)] = pair[part]
+            out = jnp.dot(ym[...], planes[p], precision=HIGHEST, preferred_element_type=F32)
             for part in range(2):
                 for k in range(2):
                     for parity in range(2):
@@ -210,12 +205,13 @@
                         where = pl.ds(k * 128 + parity, 64, stride=2)
                         ysend[f, p, part, where, :] = out[part * 64 : part * 64 + 64, lanes]
                         zbuf[f, p, col, part, where, :] = out[128 + part * 64 : 128 + part * 64 + 64, lanes]
+        for p in range(2):
             pair_copy(f, p).start()
 
     def z_step(f):
-        @pl.loop(0, 2)
-        def _(p):
+        for p in range(2):
             pair_copy(f, p).wait_recv()
+        for p in range(2):
             for (part, k), value in z_product(zbuf, zm, g_buf, f, p).items():
                 wbuf[f, part, 2 * p + k] = value
 
@@ -223,13 +219,17 @@
     def _(t):
         @pl.when(t < FIELDS)
         def _():
-            x_step(t)
+            load_u(t, 0).wait()
+            load_u(t, 1).wait()
+            x_step(t, 0)
 
             @pl.when(t == 0)
             def _():
                 pl.semaphore_wait(barrier, 10)
 
-            forward(t, 0)
+            forward(t, 0, (0, 1))
+            x_step(t, 1)
+            forward(t, 0, (2, 3))
 
         for phase in (1, 2):
 
@@ -244,7 +244,7 @@
             z_load.wait()
             g_load.wait()
 
-        @pl.when((t == 7) | (t == 8))
+        @pl.when(t == 7)
         def _():
             z_step(t - 7)
 
@@ -254,7 +254,10 @@
                 arrived(t - 6, 2, yy)
             y_step(t - 6)
 
-    z_step(FIELDS - 2)
+        @pl.when(t >= 8)
+        def _():
+            z_step(t - 7)
+
     for p in range(2):
         pair_copy(FIELDS - 1, p).wait_recv()
 
@@ -290,9 +293,9 @@
                 pltpu.VMEM((256, 256), F32),
                 pltpu.VMEM((256, 256), F32),
                 pltpu.VMEM((4, 128, 128), F32),
-                pltpu.VMEM((256, 512), F32),
+                pltpu.VMEM((2, 256, 512), F32),
                 *[pltpu.VMEM((FIELDS, 4, 4, 4, 4, 8, 128), F32)] * 4,
-                pltpu.VMEM((256, 512), F32),
+                pltpu.VMEM((2, 256, 512), F32),
                 pltpu.VMEM((FIELDS, 2, 2, 256, 128), F32),
                 pltpu.SemaphoreType.DMA((14,)),
                 pltpu.SemaphoreType.DMA((3, FIELDS, 4)),

time: 63.2 us -> 63 us (level)
  no operation moved by 1% of the time
where the time goes in v6:
time: 63 us; the launch traced here: 62.9 us
  Pallas kernels  62.2 us (99%)
  between operations  0.64 us (1%)
    pallas_call x1, Pallas kernels, local_forward(): pl.pallas_call(kernel, out_shape=(pltpu.VMEM((FIELDS, 2, 2, 2, 256, 128),...  59.4 us
    pallas_call x1, Pallas kernels, local_forward(): pl.pallas_call(last_kernel, out_shape=(out, out), in_specs=[vmem_spec] *...  2.83 us

profile of v6, /device:TPU:1, one launch (start us, length us, event | category | flops | bytes accessed | tf_op | source)
XLA Modules:
  0.0 62.9 jit_solution(4157917495630622010)
XLA Ops:
  0.6 59.4 %shard_map.86 = (f32[4,2,2,2,256,128]{5,4,3,2,1,0:T(8,128)S(1)}, f32[3,2,4,128,256]{4,3,2,1,0:T(8,128)S(1)}, f32[512,512]{1,0:T(8,128)S(1)}, f32[4,128,256]{2,1,0:T(8,128)S(1)}) custom-call(f32[4,1024,128]{2,1,0:T(8,128)} %bitcast.2, f32[4,1024,128]{2,1,0:T(8,128)} %bitcast.3, f32[4,128,256]{2,1,0:T(8,128)} %g_hbm.1, f32[256,256]{1,0:T(8,128)} %constant.8.clone.xm_hbm, ...), custom_call_target="tpu_custom_call" | custom-call | tf_op jit(solution)/shard_map/pallas_call | solution.py:281
  60.0 2.8 %shard_map.87 = (f32[4,4,128,256]{3,2,1,0:T(8,128)}, f32[4,4,128,256]{3,2,1,0:T(8,128)}) custom-call(f32[4,2,2,2,256,128]{5,4,3,2,1,0:T(8,128)S(1)} %get-tuple-element.6.zbuf, f32[3,2,4,128,256]{4,3,2,1,0:T(8,128)S(1)} %get-tuple-element.7.wbuf, f32[512,512]{1,0:T(8,128)S(1)} %get-tuple-element.8.zm, f32[4,128,256]{2,1,0:T(8,128)S(1)} %get-tuple-element.9.g_buf), custom_call_target="tpu_custom_call" | custom-call | tf_op jit(solution)/shard_map/pallas_call | solution.py:309

commit v7 on v6

--- a/solution.py
+++ b/solution.py
@@ -170,7 +170,7 @@
                 unit(yy, yy)
         for stream in range(3 if 3 in blocks else 0):
 
-            @pl.when(f % 3 == stream)
+            @pl.when((f + 2) % 3 == stream)
             def _():
                 unit(3, stream)
 

time: 63 us -> 64.1 us (1.017)
  Pallas kernels: 62.2 us -> 63.4 us
    pallas_call x1, Pallas kernels: 59.4 us -> 60.5 us  [local_forward(): pl.pallas_call(kernel, out_shape=(pltpu.VMEM((FIELDS, 2, 2, 2, 256, 128),...]
where the time goes in v7:
time: 64.1 us; the launch traced here: 64 us
  Pallas kernels  63.4 us (99%)
    pallas_call x1, Pallas kernels, local_forward(): pl.pallas_call(kernel, out_shape=(pltpu.VMEM((FIELDS, 2, 2, 2, 256, 128),...  60.5 us
    pallas_call x1, Pallas kernels, local_forward(): pl.pallas_call(last_kernel, out_shape=(out, out), in_specs=[vmem_spec] *...  2.83 us

profile of v7, /device:TPU:1, one launch (start us, length us, event | category | flops | bytes accessed | tf_op | source)
XLA Modules:
  0.0 64.0 jit_solution(6061417219176549633)
XLA Ops:
  0.6 60.5 %shard_map.86 = (f32[4,2,2,2,256,128]{5,4,3,2,1,0:T(8,128)S(1)}, f32[3,2,4,128,256]{4,3,2,1,0:T(8,128)S(1)}, f32[512,512]{1,0:T(8,128)S(1)}, f32[4,128,256]{2,1,0:T(8,128)S(1)}) custom-call(f32[4,1024,128]{2,1,0:T(8,128)} %bitcast.2, f32[4,1024,128]{2,1,0:T(8,128)} %bitcast.3, f32[4,128,256]{2,1,0:T(8,128)} %g_hbm.1, f32[256,256]{1,0:T(8,128)} %constant.8.clone.xm_hbm, ...), custom_call_target="tpu_custom_call" | custom-call | tf_op jit(solution)/shard_map/pallas_call | solution.py:281
  61.2 2.8 %shard_map.87 = (f32[4,4,128,256]{3,2,1,0:T(8,128)}, f32[4,4,128,256]{3,2,1,0:T(8,128)}) custom-call(f32[4,2,2,2,256,128]{5,4,3,2,1,0:T(8,128)S(1)} %get-tuple-element.6.zbuf, f32[3,2,4,128,256]{4,3,2,1,0:T(8,128)S(1)} %get-tuple-element.7.wbuf, f32[512,512]{1,0:T(8,128)S(1)} %get-tuple-element.8.zm, f32[4,128,256]{2,1,0:T(8,128)S(1)} %get-tuple-element.9.g_buf), custom_call_target="tpu_custom_call" | custom-call | tf_op jit(solution)/shard_map/pallas_call | solution.py:309
